TPU v7x, 128 devices: a whole 4x4x4 slice. The times are simulated.
128 devices in a mesh: gx: 8 (over y, z_lo), gy: 16 (over z_hi, x, core).
Axes of the slice: x: 4, y: 4, z: 4 (z_hi: 2, z_lo: 2; z = z_hi * 2 + z_lo), core: 2. Of those that a mesh axis runs over, the one named last changes fastest.
Arguments:
- tokens: bfloat16 [8192, 8192], P('gy', 'gx'), may hold values from -6 to 6
- pair_ids: int32 [16], replicated, may hold values from 0 to 15, each once
- query_weight: bfloat16 [8192, 8192], P('gy', 'gx'), may hold values from -0.0625 to 0.0625
- key_matrix: bfloat16 [8192, 1024], P('gy', 'gx'), may hold values from -0.0625 to 0.0625
- value_matrix: bfloat16 [8192, 1024], P('gy', 'gx'), may hold values from -0.0625 to 0.0625
- query_bias: bfloat16 [8192], P('gx'), may hold values from -13 to 13
- key_bias: bfloat16 [1024], P('gx'), may hold values from -8 to 8
- value_offset_bias: bfloat16 [1024], P('gx'), may hold values from -3 to 3
Outputs:
- attn_out: bfloat16 [8192, 8192], P('gy', 'gx')
Inputs may be any that keep to these rules, and one draw needn't show every extreme that they name: `pair_ids`: each number from 0 to 15 appears once.
All inputs are finite; a program needn't handle non-finite values.
Results may differ from a plain program's by a relative error of at most 0.0055.
The roundings to bfloat16 on the way count: a program that leaves them out, or rounds other values in their place, can miss the bound.
Values may be sent and summed in bfloat16 or wider, within the bound.
A program may use at most 128 MiB of HBM per device.

v0:
```python
import math

import jax
import jax.numpy as jnp
from jax import lax
from jax.sharding import Mesh
from jax.sharding import PartitionSpec as P

HEAD_SIZE = 128
GX = ("gx_0", "gx_1")


rope_theta = 1000000.0
neg_large = -1e30


def whole_of(shard, axes, dim):
    for axis in reversed(axes):
        shard = lax.all_gather(shard, axis, axis=dim, tiled=True)
    return shard


def side_by_side(arrays, axis, dim, along):
    ends, at = ([], 0)
    for a in arrays[:-1]:
        at += a.shape[along]
        ends.append(at)
    both = jnp.concatenate(arrays, axis=along)
    return tuple(jnp.split(lax.all_gather(both, axis, axis=dim, tiled=True), ends, axis=along))


def table_lookup(entries, wanted):
    slot_ids = lax.iota(jnp.int32, entries.shape[0])
    return jnp.sum(jnp.where(wanted[:, None] == slot_ids[None, :], entries[None, :], 0), axis=1)


def layout_positions(pair_ids, total_row_count, tok_dev):
    half_len = tok_dev // 2
    row_ids = lax.iota(jnp.int32, total_row_count)
    within = row_ids % tok_dev
    owners = table_lookup(pair_ids, row_ids // tok_dev)
    mirrored = 2 * pair_ids.shape[0] - 1 - owners
    return jnp.where(
        within < half_len, owners * half_len + within, mirrored * half_len + within - half_len
    )


def apply_rotary(values, token_positions):
    half_size = values.shape[-1] // 2
    frequency = jnp.exp(
        lax.iota(jnp.float32, half_size) * (-2.0 * math.log(rope_theta) / values.shape[-1])
    )
    angles = token_positions.astype(jnp.float32)[:, None] * frequency[None, :]
    cos_part = jnp.cos(angles)[:, None, :]
    sin_part = jnp.sin(angles)[:, None, :]
    lower_half = values[..., :half_size]
    upper_half = values[..., half_size:]
    return jnp.concatenate(
        [
            lower_half * cos_part - upper_half * sin_part,
            upper_half * cos_part + lower_half * sin_part,
        ],
        axis=-1,
    )


def absorb(running, query_block, key_block, value_block, visible):
    row_peak, totals, outputs = running
    scale = 1.0 / math.sqrt(query_block.shape[-1])
    scores = (
        jnp.einsum("hqd,khd->hqk", query_block, key_block, preferred_element_type=jnp.float32)
        * scale
    )
    if visible is not None:
        scores = jnp.where(visible[None], scores, neg_large)
    new_peak = jnp.maximum(row_peak, jnp.max(scores, axis=-1))
    weights = jnp.exp(scores - new_peak[..., None])
    if visible is not None:
        weights = jnp.where(visible[None], weights, 0.0)
    rescale = jnp.exp(row_peak - new_peak)
    totals = totals * rescale + jnp.sum(weights, axis=-1)
    outputs = outputs * rescale[..., None] + jnp.einsum(
        "hqk,khd->hqd",
        weights.astype(jnp.bfloat16),
        value_block,
        preferred_element_type=jnp.float32,
    )
    return (new_peak, totals, outputs)


def on_device(
    tokens,
    pair_ids,
    query_weight,
    key_matrix,
    value_matrix,
    query_bias,
    key_bias,
    value_offset_bias,
):
    tok_dev = tokens.shape[0]
    half_len = tok_dev // 2
    whole_rows = tok_dev * lax.axis_size("gy")
    kv_local = key_matrix.shape[1] // HEAD_SIZE
    q_local = query_weight.shape[1] // HEAD_SIZE
    query_group_width = q_local // kv_local
    gathered = whole_of(tokens, GX, 1)
    stacked = jnp.concatenate([query_weight, key_matrix, value_matrix], axis=1)
    projected = jnp.dot(
        gathered,
        lax.all_gather(stacked, "gy", axis=0, tiled=True),
        preferred_element_type=jnp.float32,
    )
    all_positions = layout_positions(pair_ids, whole_rows, tok_dev)
    own_index = lax.axis_index("gy")
    own_positions = lax.dynamic_slice_in_dim(all_positions, own_index * tok_dev, tok_dev, 0)
    own_pair = table_lookup(pair_ids, jnp.reshape(own_index, (1,)))[0]
    q_cols = q_local * HEAD_SIZE
    kv_cols = kv_local * HEAD_SIZE
    queries = projected[:, :q_cols] + query_bias.astype(jnp.float32)
    queries = apply_rotary(queries.reshape(tok_dev, q_local, HEAD_SIZE), own_positions).astype(
        jnp.bfloat16
    )
    projected_key_rows = projected[:, q_cols : q_cols + kv_cols] + key_bias.astype(jnp.float32)
    projected_key_rows = (
        apply_rotary(projected_key_rows.reshape(tok_dev, kv_local, HEAD_SIZE), own_positions)
        .astype(jnp.bfloat16)
        .reshape(tok_dev, kv_cols)
    )
    projected_value_rows = (
        projected[:, q_cols + kv_cols :] + value_offset_bias.astype(jnp.float32)
    ).astype(jnp.bfloat16)
    query_rows = (
        queries.reshape(tok_dev, kv_local, query_group_width, HEAD_SIZE)
        .transpose(1, 0, 2, 3)
        .reshape(kv_local, tok_dev * query_group_width, HEAD_SIZE)
    )
    row_positions = jnp.repeat(own_positions, query_group_width)
    row_total = tok_dev * query_group_width
    initial = (
        jnp.full((kv_local, row_total), neg_large, jnp.float32),
        jnp.zeros((kv_local, row_total), jnp.float32),
        jnp.zeros((kv_local, row_total, HEAD_SIZE), jnp.float32),
    )

    def paired(running, key_shard, value_shard, earlier):
        cut_rows = half_len * query_group_width
        former = tuple((member[:, :cut_rows] for member in running))
        latter = tuple((member[:, cut_rows:] for member in running))
        query_former = query_rows[:, :cut_rows]
        query_latter = query_rows[:, cut_rows:]
        latter = absorb(latter, query_latter, key_shard[:half_len], value_shard[:half_len], None)
        picked_state = tuple(
            (jnp.where(earlier, left, right) for left, right in zip(former, latter))
        )
        query_pick = jnp.where(earlier, query_former, query_latter)
        key_pick = jnp.where(earlier, key_shard[:half_len], key_shard[half_len:])
        value_pick = jnp.where(earlier, value_shard[:half_len], value_shard[half_len:])
        updated = absorb(picked_state, query_pick, key_pick, value_pick, None)
        former = tuple((jnp.where(earlier, fresh, kept) for fresh, kept in zip(updated, former)))
        latter = tuple((jnp.where(earlier, kept, fresh) for fresh, kept in zip(updated, latter)))
        return tuple(
            (jnp.concatenate([left, right], axis=1) for left, right in zip(former, latter))
        )

    key_piece, value_piece = side_by_side((projected_key_rows, projected_value_rows), "gy", 0, 1)
    total_row_count = key_piece.shape[0]

    def one_shard(shard_index, carried):
        begin = shard_index * tok_dev
        key_shard = lax.dynamic_slice_in_dim(key_piece, begin, tok_dev, 0).reshape(
            tok_dev, kv_local, HEAD_SIZE
        )
        value_shard = lax.dynamic_slice_in_dim(value_piece, begin, tok_dev, 0).reshape(
            tok_dev, kv_local, HEAD_SIZE
        )
        source = jnp.reshape(begin // tok_dev, (1,))
        their_pair = table_lookup(pair_ids, source)[0]

        def itself(state_in):
            key_positions = lax.dynamic_slice_in_dim(all_positions, begin, tok_dev, 0)
            visible = key_positions[None, :] <= row_positions[:, None]
            return absorb(state_in, query_rows, key_shard, value_shard, visible)

        def elsewhere(state_in):
            return paired(state_in, key_shard, value_shard, their_pair < own_pair)

        return lax.cond(their_pair == own_pair, itself, elsewhere, carried)

    row_peak, totals, outputs = lax.fori_loop(0, total_row_count // tok_dev, one_shard, initial)
    normalized = (outputs / totals[..., None]).astype(jnp.bfloat16)
    return (
        normalized.reshape(kv_local, tok_dev, query_group_width, HEAD_SIZE)
        .transpose(1, 0, 2, 3)
        .reshape(tok_dev, q_cols)
    )


def solution(mesh):
    split = Mesh(mesh.devices.reshape(4, 2, mesh.shape["gy"]), ("gx_0", "gx_1", "gy"))
    placed = (P("gy", GX), P(), P("gy", GX), P("gy", GX), P("gy", GX), P(GX), P(GX), P(GX))
    return jax.shard_map(
        on_device, mesh=split, in_specs=placed, out_specs=P("gy", GX), check_vma=False
    )
```

profile of v0, /device:TPU:1, one launch (start us, length us, event | category | flops | bytes accessed | tf_op | source)
XLA Modules:
  0.0 517.3 jit_solution(9744173479804788758)
XLA Ops:
  7.3 40.4 %all-gather.7.cloned.1.call-done = bf16[512,2048]{1,0:T(8,128)(2,1)} async-done(((bf16[512,1024]{1,0:T(8,128)(2,1)}), bf16[512,2048]{1,0:T(8,128)(2,1)}) %all-gather.7.cloned.1.call-update) | async-done | bytes 2097168 | tf_op jit(solution)/shard_map/all_gather | solution.py:19
  50.7 82.8 %all-gather.9.cloned.1.call-done = bf16[512,8192]{1,0:T(8,128)(2,1)} async-done(((bf16[512,2048]{1,0:T(8,128)(2,1)}), bf16[512,8192]{1,0:T(8,128)(2,1)}) %all-gather.9.cloned.1.call-update) | async-done | bytes 8388624 | tf_op jit(solution)/shard_map/all_gather | solution.py:19
  133.5 133.1 %all-gather.5.cloned.1.call-done = bf16[8192,1280]{1,0:T(8,128)(2,1)} async-done(((bf16[512,1280]{1,0:T(8,128)(2,1)}), bf16[8192,1280]{1,0:T(8,128)(2,1)}) %all-gather.5.cloned.1.call-update) | async-done | bytes 20971536 | tf_op jit(solution)/shard_map/all_gather | solution.py:111
  266.6 16.5 %convolution_bitcast_fusion.3 = f32[512,1280]{0,1:T(8,128)S(1)} fusion(bf16[8192,1280]{1,0:T(8,128)(2,1)} %all-gather.5.cloned.1.call-done, bf16[512,8192]{1,0:T(8,128)(2,1)} %all-gather.9.cloned.1.call-done), kind=kOutput, calls=%fused_computation.79 | convolution fusion | flops 10737418240 | bytes 31981568 | tf_op jit(solution)/shard_map/dot_general | solution.py:109
  288.5 52.3 %all-gather.11.cloned.1.call-done = bf16[8192,256]{0,1:T(8,128)(2,1)} async-done(((bf16[512,256]{0,1:T(8,128)(2,1)}), bf16[8192,256]{0,1:T(8,128)(2,1)}) %all-gather.11.cloned.1.call-update) | async-done | bytes 4194320 | tf_op jit(solution)/shard_map/all_gather | solution.py:29
  340.8 4.6 fusion.78
  346.2 161.8 %while.20 = (s32[]{:T(128)}, f32[1,4096]{1,0:T(1,128)S(1)}, f32[1,4096]{1,0:T(1,128)}, f32[1,4096,128]{2,1,0:T(8,128)S(1)}, s32[16]{0:T(128)}, /*index=5*/s32[]{...) while((s32[]{:T(128)}, f32[1,4096]{1,0:T(1,128)S(1)}, ...), condition=%wide.region_12.13_spmd.clone, body=%wide.region_2.12_spmd.clone.sunk | while | flops 1108353152 | bytes 32822028 | solution.py:190
  350.0 5.1 conditional.3
  359.6 13.9 %conditional.3 = (f32[1,4096]{1,0:T(1,128)}, f32[1,4096]{1,0:T(1,128)}, f32[1,4096,128]{2,1,0:T(8,128)S(1)}) conditional(s32[]{:T(128)} %convert_element_type.72, (s32[]{:T(128)}, s32[]{:T(128)}, f32[1,4096]{1,0:T(1,128)S(1)}, bf16[1,4096,128]{2,1,0:T(8,128)(2,1)S(1)}, bf16[512,1,128]{2,0,1:T(8,128)(2,1)S(1)}, /*index=5*/f32[1,4096]{1,0:T(1,128)}, ...), branch_computations={%region_4.8_spmd, %region_9.11_spmd} | conditional | flops 1108353024 | bytes 31740106 | solution.py:188
  369.4 4.0 fusion.39
  377.9 5.1 conditional.3
  387.5 5.1 conditional.3
  397.1 5.1 conditional.3
  406.6 5.1 conditional.3
  416.2 5.1 conditional.3
  425.7 5.1 conditional.3
  435.3 5.1 conditional.3
  444.9 5.1 conditional.3
  454.4 5.1 conditional.3
  464.0 5.1 conditional.3
  473.5 5.1 conditional.3
  483.1 5.1 conditional.3
  492.7 5.1 conditional.3
  502.2 5.1 conditional.3
  (340 shorter events, 131.6 us)
Async XLA Ops:
  6.5 41.3 %copy-start.5 = (bf16[512,1024]{1,0:T(8,128)(2,1)S(1)}, bf16[512,1024]{1,0:T(8,128)(2,1)}, u32[]{:S(2)}) copy-start(bf16[512,1024]{1,0:T(8,128)(2,1)} %param.14) | copy-start | bytes 3145732
  6.5 41.3 %copy-start.8 = (bf16[512,128]{1,0:T(8,128)(2,1)S(1)}, bf16[512,128]{1,0:T(8,128)(2,1)}, u32[]{:S(2)}) copy-start(bf16[512,128]{1,0:T(8,128)(2,1)} %param.15) | copy-start | bytes 393220
  6.5 41.3 %copy-start.7 = (bf16[512,128]{1,0:T(8,128)(2,1)S(1)}, bf16[512,128]{1,0:T(8,128)(2,1)}, u32[]{:S(2)}) copy-start(bf16[512,128]{1,0:T(8,128)(2,1)} %param.16) | copy-start | bytes 393220
  6.5 41.2 %all-gather.7.cloned.1.call-start = ((), (), s32[]{:S(2)}) async-start(), calls=%async_computation.1 | async-start | bytes 3145728 | tf_op jit(solution)/shard_map/all_gather | solution.py:19
  7.3 126.2 %all-gather.9.cloned.1.call-start = ((), (), s32[]{:S(2)}) async-start(), calls=%async_computation.2 | async-start | bytes 10485760 | tf_op jit(solution)/shard_map/all_gather | solution.py:19
  47.8 1.4 copy-start.12
  47.8 1.4 copy-start.13
  47.8 1.4 copy-start.11
  47.8 218.8 %all-gather.5.cloned.1.call-start = ((), (), s32[]{:S(2)}) async-start(), calls=%async_computation | async-start | bytes 22282240 | tf_op jit(solution)/shard_map/all_gather | solution.py:111
  49.1 291.7 %all-gather.11.cloned.1.call-start = ((), (), s32[]{:S(2)}) async-start(), calls=%async_computation.3 | async-start | bytes 4456448 | tf_op jit(solution)/shard_map/all_gather | solution.py:29
  283.1 1.4 copy-start.10
  352.1 0.7 copy-start.1
  359.6 1.4 copy-start
  362.5 2.9 copy-start.4
  362.5 2.9 copy-start.6
  365.4 3.2 copy-start.2
  369.4 4.0 copy-start.3
  380.1 0.7 copy-start.1
  389.6 0.7 copy-start.1
  399.2 0.7 copy-start.1
  408.7 0.7 copy-start.1
  418.3 0.7 copy-start.1
  427.9 0.7 copy-start.1
  437.4 0.7 copy-start.1
  (8 other events, 5.6 us)
Sparse Core Ops, SparseCore 0:
  9.0 38.7 all-gather.6
  49.4 84.0 all-gather.8
  135.9 130.6 all-gather.4
  284.7 56.0 all-gather.10
where the time goes:
time: 521 us; the launch traced here: 517 us
  waiting for transfers between devices  309 us (59%)
  matrix products  56.3 us (11%)
  other arithmetic  55.3 us (11%)
  local copies, waits for them, and re-layouts  44.3 us (9%)
  loops' own time  38.5 us (7%)
  between operations  13.4 us (3%)
    all_gather x1, waiting for transfers between devices, on_device(): lax.all_gather(stacked, 'gy', axis=0, tiled=True)  133 us
    all_gather x2, waiting for transfers between devices, whole_of(): shard = lax.all_gather(shard, axis, axis=dim, tiled=True)  123 us
    all_gather x1, waiting for transfers between devices, side_by_side(): lax.all_gather(both, axis, axis=dim, tiled=True)  52.3 us
    dot_general x31, matrix products, absorb(): jnp.einsum('hqk,khd->hqd', weights.astype(jnp.bfloat16), value_block, pre...  24.1 us
    reduce_sum x18, other arithmetic, table_lookup(): jnp.sum(jnp.where(wanted[:, None] == slot_ids[None, :], entries[None, :],...  22 us
    another operation x1, loops' own time, on_device(): lax.fori_loop(0, total_row_count // tok_dev, one_shard, initial)  19.6 us
    another operation x16, loops' own time, one_shard(): return lax.cond(their_pair == own_pair, itself, elsewhere, carried)  18.9 us
    dynamic_slice x32, local copies, waits for them, and re-layouts, one_shard(): lax.dynamic_slice_in_dim(value_piece, begin, tok_dev, 0)  17.7 us
  transfers between devices with their start and end apart: 4, of which 4 were waited for; matrix products, arithmetic and copies ran while one was open for 1% of the time, Pallas kernels for 0%

commit v1 on v0

v1 whole, which is shorter than its diff:
```python
import functools
import math

import jax
import jax.numpy as jnp
from jax import lax
from jax.experimental import pallas as pl
from jax.experimental.pallas import tpu as pltpu
from jax.sharding import PartitionSpec as P

THETA = 1000000.0
EXP2_SCALE = math.log2(math.e) / math.sqrt(128)
NEG = -1e30
MESH = pl.DeviceIdType.MESH

XS = 4
SLOTS = 7
S_E, S_L = 5, 6
KT = 1024
VIA_Z = (4, 16)


def kernel(
    pair_ref, x_hbm, wq_hbm, wk_hbm, wv_hbm, bq_ref, bk_ref, bv_ref,
    q_out, kv_out, m_out, l_out, o_out,
    xb, wb, kvb, qs, acc, cos_t, sin_t, st_m, st_l, st_o, loc_sem, out_sem, ws, wr, xs, xr,
):
    gx, gy = lax.axis_index("gx"), lax.axis_index("gy")
    y, zl = gx // 2, gx % 2
    zh, x, c = gy // 8, (gy // 2) % 4, gy % 2

    def at(dx=0, dy=0, dzh=0, dzl=0, dc=0):
        return (
            ((y + dy) % 4) * 2 + (zl + dzl) % 2,
            (((zh + dzh) % 2) * 4 + (x + dx) % 4) * 2 + (c + dc) % 2,
        )

    core, xp, xm, yp, ym, zfar, znear = (
        at(dc=1), at(dx=1), at(dx=3), at(dy=1), at(dy=3), at(dzh=1), at(dzl=1)
    )

    def block(plane, dx, dc=0):
        return (((zh + plane) % 2) * 4 + (x + dx) % 4) * 2 + (c + dc) % 2

    def xblock(plane, dy):
        return ((y + dy) % 4) * 2 + (zl + plane) % 2

    local = []

    def load(src, dst, n):
        cp = pltpu.make_async_copy(src, dst, loc_sem.at[n])
        cp.start()
        local.append(cp)

    load(wk_hbm, wb.at[0, gy, :, pl.ds(0, 128)], 0)
    load(wv_hbm, wb.at[0, gy, :, pl.ds(128, 128)], 1)
    for r in range(XS):
        load(x_hbm.at[pl.ds(r * 128, 128)], xb.at[r, gx], 2 + r)
    for t in range(1, 5):
        load(wq_hbm.at[:, pl.ds((t - 1) * 256, 256)], wb.at[t, gy], 5 + t)

    barrier = pltpu.get_barrier_semaphore()
    for n in (core, xp, xm, yp, ym, zfar, znear):
        pl.semaphore_signal(barrier, inc=1, device_id=n, device_id_type=MESH)
    pl.semaphore_wait(barrier, 7)

    sends = []

    def send(src, dst, ssem, rsem, dev):
        cp = pltpu.make_async_remote_copy(
            src_ref=src, dst_ref=dst, send_sem=ssem, recv_sem=rsem, device_id=dev,
            device_id_type=MESH,
        )
        cp.start()
        sends.append(cp)

    def arrived(ref, sem):
        pltpu.make_async_copy(ref, ref, sem).wait()

    def blk(s, j):
        return wb.at[s, j] if s < S_E else kvb.at[s - S_E, j]

    def cuts(s):
        n = 512 if s < S_E else 256
        v = n * VIA_Z[0] // VIA_Z[1]
        return pl.ds(0, n // 2), pl.ds(n // 2, n // 2), pl.ds(0, n - v), pl.ds(n - v, v)

    P0, OM, OP, PM, PP, PMV, PPV, O2A, O2B, P2A, P2B, D = range(12)
    doff = {(0, 0): 0, (0, 3): 1, (0, 1): 2, (1, 0): 3, (1, 3): 4, (1, 1): 5, (0, 2): 6, (1, 2): 7}

    def wsend(s, ref, role, dev):
        send(ref, ref, ws.at[s, role], wr.at[s, role], dev)

    def d2d(s, plane, dx):
        wsend(s, blk(s, block(plane, dx)), D + doff[(plane, dx)], core)

    def own(s):
        b = blk(s, gy)
        wsend(s, b, P0, zfar)
        wsend(s, b, OM, xp)
        wsend(s, b, OP, xm)
        d2d(s, 0, 0)

    def relay_own(s):
        lo, hi, u, v = cuts(s)
        b = blk(s, block(0, 3))
        arrived(b, wr.at[s, OM])
        wsend(s, b.at[lo], O2A, xp)
        wsend(s, b.at[v], PMV, zfar)
        d2d(s, 0, 3)
        b = blk(s, block(0, 1))
        arrived(b, wr.at[s, OP])
        wsend(s, b.at[hi], O2B, xm)
        wsend(s, b.at[v], PPV, zfar)
        d2d(s, 0, 1)

    def partner(s):
        lo, hi, u, v = cuts(s)
        b = blk(s, block(1, 0))
        arrived(b, wr.at[s, P0])
        wsend(s, b.at[u], PM, xp)
        wsend(s, b.at[u], PP, xm)
        d2d(s, 1, 0)

    def relay_partner(s):
        lo, hi, u, v = cuts(s)
        b = blk(s, block(1, 3))
        arrived(b.at[u], wr.at[s, PM])
        arrived(b.at[v], wr.at[s, PMV])
        wsend(s, b.at[lo], P2A, xp)
        d2d(s, 1, 3)
        b = blk(s, block(1, 1))
        arrived(b.at[u], wr.at[s, PP])
        arrived(b.at[v], wr.at[s, PPV])
        wsend(s, b.at[hi], P2B, xm)
        d2d(s, 1, 1)

    def last(s):
        lo, hi, u, v = cuts(s)
        for plane, ra, rb in ((0, O2A, O2B), (1, P2A, P2B)):
            b = blk(s, block(plane, 2))
            arrived(b.at[lo], wr.at[s, ra])
            arrived(b.at[hi], wr.at[s, rb])
            d2d(s, plane, 2)

    def other_core(s):
        for (plane, dx), d in doff.items():
            arrived(blk(s, block(plane, dx, 1)), wr.at[s, D + d])

    XZ, XOM, XOP, XPM, XPP, XO2A, XO2B, XP2A, XP2B = range(9)
    xlo, xhi = pl.ds(0, 64), pl.ds(64, 64)

    def xsend(t, ref, role, dev):
        send(ref, ref, xs.at[t, role], xr.at[t, role], dev)

    def xown(t):
        b = xb.at[t, gx]
        xsend(t, b, XZ, znear)
        xsend(t, b, XOM, yp)
        xsend(t, b, XOP, ym)

    def xrelay(t, plane):
        rm, rp, ra, rb = (XOM, XOP, XO2A, XO2B) if plane == 0 else (XPM, XPP, XP2A, XP2B)
        b = xb.at[t, xblock(plane, 3)]
        arrived(b, xr.at[t, rm])
        xsend(t, b.at[xlo], ra, yp)
        b = xb.at[t, xblock(plane, 1)]
        arrived(b, xr.at[t, rp])
        xsend(t, b.at[xhi], rb, ym)

    def xpartner(t):
        b = xb.at[t, xblock(1, 0)]
        arrived(b, xr.at[t, XZ])
        xsend(t, b, XPM, yp)
        xsend(t, b, XPP, ym)

    def xlast(t):
        for plane, ra, rb in ((0, XO2A, XO2B), (1, XP2A, XP2B)):
            b = xb.at[t, xblock(plane, 2)]
            arrived(b.at[xlo], xr.at[t, ra])
            arrived(b.at[xhi], xr.at[t, rb])

    def project(s, half):
        total = None
        for b in range(8):
            part = jnp.dot(
                xb[pl.ds(2 * half, 2), b].reshape(256, 1024),
                wb[s, pl.ds(2 * b, 2)].reshape(1024, 256),
                preferred_element_type=jnp.float32,
            )
            total = part if total is None else total + part
        acc[...] = total

    def rope(u, half):
        r = pl.ds(half * 256, 256)
        return u * cos_t[r, :] + pltpu.roll(u, 64, 1) * sin_t[r, :]

    def make_kv(half):
        project(0, half)
        kvb[half, gy, :, 0:128] = rope(
            acc[:, 0:128] + bk_ref[...].astype(jnp.float32), half
        ).astype(jnp.bfloat16)
        kvb[half, gy, :, 128:256] = (
            acc[:, 128:256] + bv_ref[...].astype(jnp.float32)
        ).astype(jnp.bfloat16)

    def make_q(hp, half):
        project(hp + 1, half)
        for g in range(2):
            h = 2 * hp + g
            u = acc[:, g * 128:(g + 1) * 128] + bq_ref[:, h * 128:(h + 1) * 128].astype(jnp.float32)
            qs[half, pl.ds(h * 256, 256), :] = rope(u, half).astype(jnp.bfloat16)

    def tables():
        p = pair_ref[gy]
        row = lax.broadcasted_iota(jnp.int32, (512, 128), 0)
        pos = jnp.where(row < 256, p * 256 + row, (31 - p) * 256 + row - 256)
        lane = lax.broadcasted_iota(jnp.int32, (512, 128), 1)
        half = (lane % 64).astype(jnp.float32)
        freq = jnp.exp(half * (-2.0 * math.log(THETA) / 128))
        ang = pos.astype(jnp.float32) * freq
        cos_t[...] = jnp.cos(ang)
        s = jnp.sin(ang)
        sin_t[...] = jnp.where(lane < 64, -s, s)

    outs = []

    def put(src, dst, n):
        cp = pltpu.make_async_copy(src, dst, out_sem.at[n])
        cp.start()
        outs.append(cp)

    def put_kv(half):
        put(kvb.at[half], kv_out.at[half], half)

    def put_state(hp):
        put(st_m.at[hp], m_out.at[hp], 3 + hp)
        put(st_l.at[hp], l_out.at[hp], 7 + hp)
        put(st_o.at[hp], o_out.at[hp], 11 + hp)

    def attend(hp):
        q = qs[1, pl.ds(hp * 512, 512), :]
        carry = (
            jnp.full((512, 1), NEG, jnp.float32),
            jnp.zeros((512, 128), jnp.float32),
            jnp.zeros((512, 128), jnp.float32),
        )
        m, l, o = lax.fori_loop(0, 4, lambda t, st: absorb(q, kvb, 0, t, st, None), carry)
        st_m[hp] = jnp.broadcast_to(m, (512, 128))
        st_l[hp] = l
        st_o[hp] = o

    local[0].wait()
    local[1].wait()
    own(0)
    local[2].wait()
    xown(0)
    for cp in local[3:]:
        cp.wait()
    tables()
    own(1)
    xown(1)
    relay_own(0)
    xrelay(0, 0)
    xpartner(0)
    partner(0)
    own(2)
    xown(2)
    xrelay(0, 1)
    xrelay(1, 0)
    xpartner(1)
    relay_partner(0)
    relay_own(1)
    partner(1)
    last(0)
    xlast(0)
    own(3)
    xown(3)
    xrelay(1, 1)
    xrelay(2, 0)
    xpartner(2)
    relay_partner(1)
    relay_own(2)
    partner(2)
    other_core(0)
    xlast(1)
    make_kv(0)
    last(1)
    own(S_E)
    xrelay(2, 1)
    xrelay(3, 0)
    xpartner(3)
    relay_partner(2)
    relay_own(3)
    relay_own(S_E)
    partner(S_E)
    partner(3)
    own(4)
    other_core(1)
    make_q(0, 0)
    xrelay(3, 1)
    last(2)
    xlast(2)
    relay_partner(S_E)
    relay_partner(3)
    other_core(2)
    make_q(1, 0)
    relay_own(4)
    partner(4)
    last(S_E)
    other_core(S_E)
    put_kv(0)
    xlast(3)
    make_kv(1)
    last(3)
    make_q(0, 1)
    own(S_L)
    relay_partner(4)
    make_q(1, 1)
    other_core(3)
    make_q(2, 0)
    relay_own(S_L)
    partner(S_L)
    make_q(2, 1)
    attend(0)
    relay_partner(S_L)
    last(4)
    attend(1)
    last(S_L)
    put_state(0)
    attend(2)
    other_core(4)
    make_q(3, 0)
    make_q(3, 1)
    other_core(S_L)
    put_kv(1)
    put_state(1)
    attend(3)
    put_state(2)
    put_state(3)
    put(qs, q_out, 2)
    for cp in sends:
        cp.wait_send()
    for cp in outs:
        cp.wait()


def absorb(q, kv, seg, t, state, vis):
    m, l, o = state
    kt = kv[seg, pl.ds(t * 4, 4), :, 0:128].reshape(KT, 128)
    vt = kv[seg, pl.ds(t * 4, 4), :, 128:256].reshape(KT, 128)
    s = lax.dot_general(q, kt, (((1,), (1,)), ((), ())), preferred_element_type=jnp.float32)
    if vis is not None:
        s = jnp.where(vis, s, NEG)
    mx = s[:, 0:128]
    for u in range(1, KT // 128):
        mx = jnp.maximum(mx, s[:, u * 128:(u + 1) * 128])
    mnew = jnp.maximum(m, jnp.max(mx, axis=1, keepdims=True) * EXP2_SCALE)
    pr = jnp.exp2(s * EXP2_SCALE - mnew)
    a = jnp.exp2(m - mnew)
    ps = pr[:, 0:128]
    for u in range(1, KT // 128):
        ps = ps + pr[:, u * 128:(u + 1) * 128]
    l = l * a + ps
    o = o * a + jnp.dot(pr.astype(jnp.bfloat16), vt, preferred_element_type=jnp.float32)
    return mnew, l, o


def gather_project(pair_ids, tokens, wq, wk, wv, bq, bk, bv):
    vmem = pl.BlockSpec(memory_space=pltpu.VMEM)
    hbm = pl.BlockSpec(memory_space=pl.ANY)
    state = jax.ShapeDtypeStruct((4, 512, 128), jnp.float32)
    return pl.pallas_call(
        kernel,
        out_shape=(
            jax.ShapeDtypeStruct((2, 2048, 128), jnp.bfloat16),
            jax.ShapeDtypeStruct((2, 16, 256, 256), jnp.bfloat16),
            state, state, state,
        ),
        in_specs=[pl.BlockSpec(memory_space=pltpu.SMEM), hbm, hbm, hbm, hbm, vmem, vmem, vmem],
        out_specs=(hbm,) * 5,
        scratch_shapes=[
            pltpu.VMEM((XS, 8, 128, 1024), jnp.bfloat16),
            pltpu.VMEM((5, 16, 512, 256), jnp.bfloat16),
            pltpu.VMEM((2, 16, 256, 256), jnp.bfloat16),
            pltpu.VMEM((2, 2048, 128), jnp.bfloat16),
            pltpu.VMEM((256, 256), jnp.float32),
            pltpu.VMEM((512, 128), jnp.float32),
            pltpu.VMEM((512, 128), jnp.float32),
            pltpu.VMEM((4, 512, 128), jnp.float32),
            pltpu.VMEM((4, 512, 128), jnp.float32),
            pltpu.VMEM((4, 512, 128), jnp.float32),
            pltpu.SemaphoreType.DMA((10,)),
            pltpu.SemaphoreType.DMA((15,)),
            pltpu.SemaphoreType.DMA((SLOTS, 19)),
            pltpu.SemaphoreType.DMA((SLOTS, 19)),
            pltpu.SemaphoreType.DMA((XS, 9)),
            pltpu.SemaphoreType.DMA((XS, 9)),
        ],
        compiler_params=pltpu.CompilerParams(
            collective_id=0, has_side_effects=True, vmem_limit_bytes=63 * 2**20
        ),
    )(pair_ids, tokens, wq, wk, wv, bq.reshape(1, -1), bk.reshape(1, -1), bv.reshape(1, -1))


def attn_kernel(pair_ref, q_hbm, kv_hbm, m_hbm, l_hbm, o_hbm, out_ref, q, kv, m0, l0, o0, sem, *, G):
    def cp(half, j):
        slot = pair_ref[j] if half == 0 else 15 - pair_ref[j]
        return pltpu.make_async_copy(kv_hbm.at[half, j], kv.at[half, slot], sem.at[half, j])

    rest = [
        pltpu.make_async_copy(a, b, sem.at[2, n])
        for n, (a, b) in enumerate(
            ((q_hbm.at[0], q.at[0]), (q_hbm.at[1], q.at[1]), (m_hbm, m0), (l_hbm, l0), (o_hbm, o0))
        )
    ]
    rest[0].start()
    for half in range(2):

        @pl.loop(0, 16)
        def _(j):
            cp(half, j).start()

        for r in rest[1:] if half else ():
            r.start()
    p = pair_ref[lax.axis_index("gy")]
    R = G * 256
    for half in range(2):

        @pl.loop(0, 16)
        def _(j):
            cp(half, j).wait()

        for r in rest[1:] if half else rest[:1]:
            r.wait()
        blk = p if half == 0 else 15 - p
        full = blk // 4

        @pl.loop(0, 8 // G)
        def _(i):
            rows = pl.ds(pl.multiple_of(i * R, R), R)
            qt = q[half, rows, :]
            if half:
                parts = [
                    jnp.concatenate([r[i * (G // 2) + g] for g in range(G // 2)], axis=0)
                    for r in (m0, l0, o0)
                ]
                state = (parts[0][:, 0:1], parts[1], parts[2])
            else:
                state = (
                    jnp.full((R, 1), NEG, jnp.float32),
                    jnp.zeros((R, 128), jnp.float32),
                    jnp.zeros((R, 128), jnp.float32),
                )
            ahead = lax.broadcasted_iota(jnp.int32, (R, KT), 1) - (
                lax.broadcasted_iota(jnp.int32, (R, KT), 0) % 256
            )
            state = absorb(qt, kv, half, full, state, ahead <= (blk - full * 4) * 256)
            m, l, o = lax.fori_loop(
                0, full, lambda t, st: absorb(qt, kv, half, t, st, None), state
            )
            o = (o / jnp.sum(l, axis=1, keepdims=True)).astype(jnp.bfloat16)
            for g in range(G):
                out_ref[half * 256:(half + 1) * 256, pl.ds(pl.multiple_of((i * G + g) * 128, 128), 128)] = (
                    o[g * 256:(g + 1) * 256]
                )


def on_device(tokens, pair_ids, wq, wk, wv, bq, bk, bv):
    q, kv, m, l, o = gather_project(pair_ids, tokens, wq, wk, wv, bq, bk, bv)
    hbm = pl.BlockSpec(memory_space=pl.ANY)
    return pl.pallas_call(
        functools.partial(attn_kernel, G=4),
        out_shape=jax.ShapeDtypeStruct((512, 1024), jnp.bfloat16),
        in_specs=[pl.BlockSpec(memory_space=pltpu.SMEM)] + [hbm] * 5,
        out_specs=pl.BlockSpec(memory_space=pltpu.VMEM),
        scratch_shapes=[
            pltpu.VMEM((2, 2048, 128), jnp.bfloat16),
            pltpu.VMEM((2, 16, 256, 256), jnp.bfloat16),
            pltpu.VMEM((4, 512, 128), jnp.float32),
            pltpu.VMEM((4, 512, 128), jnp.float32),
            pltpu.VMEM((4, 512, 128), jnp.float32),
            pltpu.SemaphoreType.DMA((3, 16)),
        ],
        compiler_params=pltpu.CompilerParams(vmem_limit_bytes=60 * 2**20),
    )(pair_ids, q, kv, m, l, o)


def solution(mesh):
    placed = (P("gy", "gx"), P(), P("gy", "gx"), P("gy", "gx"), P("gy", "gx"), P("gx"), P("gx"), P("gx"))
    return jax.shard_map(
        on_device, mesh=mesh, in_specs=placed, out_specs=P("gy", "gx"), check_vma=False
    )
```

time: 521 us -> 153 us (0.29)
  waiting for transfers between devices: 309 us -> 0 us
  Pallas kernels: 0 us -> 151 us
  matrix products: 56.3 us -> 0 us
  other arithmetic: 55.3 us -> 0 us
  local copies, waits for them, and re-layouts: 44.3 us -> 1.28 us
  loops' own time: 38.5 us -> 0 us
  between operations: 13.4 us -> 0.19 us
    all_gather x4 -> x0, waiting for transfers between devices: 309 us -> none  [the longest x1 133 us: on_device(): lax.all_gather(stacked, 'gy', axis=0, tiled=True)]
    pallas_call x0 -> x2, Pallas kernels: none -> 151 us  [the longest x1 124 us: gather_project(): pl.pallas_call(kernel, out_shape=(jax.ShapeDtypeStruct((2, 2048, 128), jn...]
    dot_general x63 -> x0, matrix products: 56.3 us -> none  [the longest x31 24.1 us: absorb(): jnp.einsum('hqk,khd->hqd', weights.astype(jnp.bfloat16), value_block, pre...]
    another operation x17 -> x0, loops' own time: 38.5 us -> none  [the longest x1 19.6 us: on_device(): lax.fori_loop(0, total_row_count // tok_dev, one_shard, initial)]
    reduce_sum x49 -> x0, other arithmetic: 34.4 us -> none  [the longest x18 22 us: table_lookup(): jnp.sum(jnp.where(wanted[:, None] == slot_ids[None, :], entries[None, :],...]
    dynamic_slice x49 -> x0, local copies, waits for them, and re-layouts: 21 us -> none  [the longest x32 17.7 us: one_shard(): lax.dynamic_slice_in_dim(value_piece, begin, tok_dev, 0)]
    concatenate x34 -> x0, other arithmetic: 14.7 us -> none  [the longest x30 11.7 us: paired(): jnp.concatenate([left, right], axis=1)]
    while x16 -> x0, local copies, waits for them, and re-layouts: 11.5 us -> none
  transfers between devices with their start and end apart: 4 -> 0, of which waited for: 4 -> 0; matrix products, arithmetic and copies ran while one was open for 1% -> 0% of each run, Pallas kernels for 0% -> 0%
where the time goes in v1:
time: 153 us
  Pallas kernels  151 us (99%)
    pallas_call x1, Pallas kernels, gather_project(): pl.pallas_call(kernel, out_shape=(jax.ShapeDtypeStruct((2, 2048, 128), jn...  124 us
    pallas_call x1, Pallas kernels, on_device(): pl.pallas_call(functools.partial(attn_kernel, G=4), out_shape=jax.ShapeDt...  26.8 us

profile of v1, /device:TPU:1, one launch (start us, length us, event | category | flops | bytes accessed | tf_op | source)
XLA Modules:
  0.0 152.7 jit_solution(8308228294378856724)
XLA Ops:
  0.0 1.3 reshape.9.bq_ref
  1.3 124.5 %shard_map.82 = (bf16[2,2048,128]{2,1,0:T(8,128)(2,1)}, bf16[2,16,256,256]{3,2,1,0:T(8,128)(2,1)}, f32[4,512,128]{2,1,0:T(8,128)}, f32[4,512,128]{2,1,0:T(8,128)}, f32[4,512,128]{2,1,0:T(8,128)}) custom-call(s32[16]{0:T(128)} %pair_ref.3, bf16[512,1024]{1,0:T(8,128)(2,1)} %x_hbm.1, bf16[512,1024]{1,0:T(8,128)(2,1)} %wq_hbm.1, bf16[512,128]{1,0:T(8,128)(2,1)} %wk_hbm.1, ...), custom_call_target="tpu_custom_call" | custom-call | tf_op jit(solution)/shard_map/pallas_call | solution.py:373
  125.7 26.8 %shard_map.83 = bf16[512,1024]{1,0:T(8,128)(2,1)} custom-call(s32[16]{0:T(128)} %pair_ref.3, bf16[2,2048,128]{2,1,0:T(8,128)(2,1)} %get-tuple-element.10.q_hbm, bf16[2,16,256,256]{3,2,1,0:T(8,128)(2,1)} %get-tuple-element.11.kv_hbm, f32[4,512,128]{2,1,0:T(8,128)} %get-tuple-element.12.m_hbm, f32[4,512,128]{2,1,0:T(8,128)} %get-tuple-element.13.l_hbm, ...), custom_call_target="tpu_custom_call" | custom-call | tf_op jit(solution)/shard_map/pallas_call | solution.py:472

commit v2 on v1

--- a/solution.py
+++ b/solution.py
@@ -198,17 +198,17 @@
     def make_kv(half):
         project(0, half)
         kvb[half, gy, :, 0:128] = rope(
-            acc[:, 0:128] + bk_ref[...].astype(jnp.float32), half
+            acc[:, 0:128] + bk_ref[...].astype(jnp.float32).reshape(1, 128), half
         ).astype(jnp.bfloat16)
         kvb[half, gy, :, 128:256] = (
-            acc[:, 128:256] + bv_ref[...].astype(jnp.float32)
+            acc[:, 128:256] + bv_ref[...].astype(jnp.float32).reshape(1, 128)
         ).astype(jnp.bfloat16)
 
     def make_q(hp, half):
         project(hp + 1, half)
         for g in range(2):
             h = 2 * hp + g
-            u = acc[:, g * 128:(g + 1) * 128] + bq_ref[:, h * 128:(h + 1) * 128].astype(jnp.float32)
+            u = acc[:, g * 128:(g + 1) * 128] + bq_ref[h * 128:(h + 1) * 128].astype(jnp.float32).reshape(1, 128)
             qs[half, pl.ds(h * 256, 256), :] = rope(u, half).astype(jnp.bfloat16)
 
     def tables():
@@ -400,7 +400,7 @@
         compiler_params=pltpu.CompilerParams(
             collective_id=0, has_side_effects=True, vmem_limit_bytes=63 * 2**20
         ),
-    )(pair_ids, tokens, wq, wk, wv, bq.reshape(1, -1), bk.reshape(1, -1), bv.reshape(1, -1))
+    )(pair_ids, tokens, wq, wk, wv, bq, bk, bv)
 
 
 def attn_kernel(pair_ref, q_hbm, kv_hbm, m_hbm, l_hbm, o_hbm, out_ref, q, kv, m0, l0, o0, sem, *, G):

time: 153 us -> 153 us (level); the launches traced: 153 us -> 150 us
  no operation moved by 1% of the time
where the time goes in v2:
time: 153 us; the launch traced here: 150 us
  Pallas kernels  150 us (98%)
    pallas_call x1, Pallas kernels, gather_project(): pl.pallas_call(kernel, out_shape=(jax.ShapeDtypeStruct((2, 2048, 128), jn...  124 us
    pallas_call x1, Pallas kernels, on_device(): pl.pallas_call(functools.partial(attn_kernel, G=4), out_shape=jax.ShapeDt...  25.7 us

profile of v2, /device:TPU:1, one launch (start us, length us, event | category | flops | bytes accessed | tf_op | source)
XLA Modules:
  0.0 150.3 jit_solution(4287415525656011178)
XLA Ops:
  0.0 124.5 %shard_map.82 = (bf16[2,2048,128]{2,1,0:T(8,128)(2,1)}, bf16[2,16,256,256]{3,2,1,0:T(8,128)(2,1)}, f32[4,512,128]{2,1,0:T(8,128)}, f32[4,512,128]{2,1,0:T(8,128)}, f32[4,512,128]{2,1,0:T(8,128)}) custom-call(s32[16]{0:T(128)} %pair_ref.3, bf16[512,1024]{1,0:T(8,128)(2,1)} %x_hbm.1, bf16[512,1024]{1,0:T(8,128)(2,1)} %wq_hbm.1, bf16[512,128]{1,0:T(8,128)(2,1)} %wk_hbm.1, ...), custom_call_target="tpu_custom_call" | custom-call | tf_op jit(solution)/shard_map/pallas_call | solution.py:373
  124.5 25.7 %shard_map.83 = bf16[512,1024]{1,0:T(8,128)(2,1)} custom-call(s32[16]{0:T(128)} %pair_ref.3, bf16[2,2048,128]{2,1,0:T(8,128)(2,1)} %get-tuple-element.10.q_hbm, bf16[2,16,256,256]{3,2,1,0:T(8,128)(2,1)} %get-tuple-element.11.kv_hbm, f32[4,512,128]{2,1,0:T(8,128)} %get-tuple-element.12.m_hbm, f32[4,512,128]{2,1,0:T(8,128)} %get-tuple-element.13.l_hbm, ...), custom_call_target="tpu_custom_call" | custom-call | tf_op jit(solution)/shard_map/pallas_call | solution.py:472

commit v3 on v2

--- a/solution.py
+++ b/solution.py
@@ -332,10 +332,10 @@
     other_core(4)
     make_q(3, 0)
     make_q(3, 1)
+    put_state(1)
+    attend(3)
     other_core(S_L)
     put_kv(1)
-    put_state(1)
-    attend(3)
     put_state(2)
     put_state(3)
     put(qs, q_out, 2)

time: 153 us -> 152 us (level)
  no operation moved by 1% of the time
where the time goes in v3:
time: 152 us; the launch traced here: 150 us
  Pallas kernels  149 us (98%)
    pallas_call x1, Pallas kernels, gather_project(): pl.pallas_call(kernel, out_shape=(jax.ShapeDtypeStruct((2, 2048, 128), jn...  125 us
    pallas_call x1, Pallas kernels, on_device(): pl.pallas_call(functools.partial(attn_kernel, G=4), out_shape=jax.ShapeDt...  24.2 us

profile of v3, /device:TPU:1, one launch (start us, length us, event | category | flops | bytes accessed | tf_op | source)
XLA Modules:
  0.0 149.6 jit_solution(61745807284950685)
XLA Ops:
  0.0 125.2 %shard_map.82 = (bf16[2,2048,128]{2,1,0:T(8,128)(2,1)}, bf16[2,16,256,256]{3,2,1,0:T(8,128)(2,1)}, f32[4,512,128]{2,1,0:T(8,128)}, f32[4,512,128]{2,1,0:T(8,128)}, f32[4,512,128]{2,1,0:T(8,128)}) custom-call(s32[16]{0:T(128)} %pair_ref.3, bf16[512,1024]{1,0:T(8,128)(2,1)} %x_hbm.1, bf16[512,1024]{1,0:T(8,128)(2,1)} %wq_hbm.1, bf16[512,128]{1,0:T(8,128)(2,1)} %wk_hbm.1, ...), custom_call_target="tpu_custom_call" | custom-call | tf_op jit(solution)/shard_map/pallas_call | solution.py:373
  125.2 24.2 %shard_map.83 = bf16[512,1024]{1,0:T(8,128)(2,1)} custom-call(s32[16]{0:T(128)} %pair_ref.3, bf16[2,2048,128]{2,1,0:T(8,128)(2,1)} %get-tuple-element.10.q_hbm, bf16[2,16,256,256]{3,2,1,0:T(8,128)(2,1)} %get-tuple-element.11.kv_hbm, f32[4,512,128]{2,1,0:T(8,128)} %get-tuple-element.12.m_hbm, f32[4,512,128]{2,1,0:T(8,128)} %get-tuple-element.13.l_hbm, ...), custom_call_target="tpu_custom_call" | custom-call | tf_op jit(solution)/shard_map/pallas_call | solution.py:472
